TPU v7x, 32 devices: a whole 2x2x4 slice. The times are simulated.
32 devices in a mesh: req: 2 (over y), patch: 16 (over z, x, core).
Axes of the slice: x: 2, y: 2, z: 4, core: 2. Of those that a mesh axis runs over, the one named last changes fastest.
Arguments:
- tokens: bfloat16 [1536, 1152], P(('req', 'patch')), parts along dimension 0, may hold values from -6 to 6
- positions: int32 [2, 1536], P(None, ('req', 'patch')), parts along dimension 1, may hold values from 0 to 95
- counts: int32 [32], P('req'), parts along dimension 0, may hold values from 1 to 48, 384 in all
- timestep: int32 [2], P('req'), parts along dimension 0, may hold values from 0 to 999
- time_in: bfloat16 [256, 1152], replicated, may hold values from -0.375 to 0.375
- time_out: bfloat16 [1152, 1152], P(None, 'patch'), may hold values from -0.1875 to 0.1875
- ada_weight: bfloat16 [1152, 3456], P('patch'), may hold values from -0.375 to 0.375
- qkv_weight: bfloat16 [1152, 3456], replicated, may hold values from -2 to 2, as said below
- out_weight: bfloat16 [1152, 1152], replicated, may hold values from -0.1875 to 0.1875
Outputs:
- block_out: bfloat16 [1536, 1152], P(('req', 'patch')), parts along dimension 0
There are 2 independent parts, one for each index of `req`. A program takes and returns all parts, laid end to end along the dimension named above; an argument that names none is the same for every part. Nothing has to cross between parts.
Inputs may be any that keep to these rules, and one draw needn't show every extreme that they name: `counts`: used slots are the first ones of each block; they sum to exactly 384, and some block uses all 48. `qkv_weight`: columns are 1152 of queries, 1152 of keys, 1152 of values, each head's 72 columns side by side.
All inputs are finite; a program needn't handle non-finite values.
Results may differ from a plain program's by a relative error of at most 0.0039.
Values may be sent and summed in bfloat16 or wider, within the bound.
A program may use at most 64 MiB of HBM per device.

v0:
```python
import math
import jax
import jax.numpy as jnp
from jax import lax
from jax.sharding import PartitionSpec as P

HEADS = 16
neg_large = -1e30
key_block = 512


def time_features(timestep, freq_size):
    half_size = freq_size // 2
    frequencies = jnp.exp(-math.log(10000.0) * jnp.arange(half_size, dtype=jnp.float32) / half_size)
    angles = timestep.astype(jnp.float32)[:, None] * frequencies[None, :]
    return jnp.concatenate([jnp.cos(angles), jnp.sin(angles)], axis=1).astype(jnp.bfloat16)


def position_table(positions, model_width):
    quarter = model_width // 4
    omegas = jnp.power(10000.0, -jnp.arange(quarter, dtype=jnp.float32) / quarter)
    row_angle = positions[0].astype(jnp.float32)[:, None] * omegas[None, :]
    col_angle = positions[1].astype(jnp.float32)[:, None] * omegas[None, :]
    return jnp.concatenate(
        [jnp.sin(row_angle), jnp.cos(row_angle), jnp.sin(col_angle), jnp.cos(col_angle)], axis=1
    )


def attend_update(running, query_heads, key_piece, value_piece, mask_piece, inv_root):
    row_top, denominator, weighted = running
    key_count = key_piece.shape[0]
    head_count = query_heads.shape[1]
    head_size = query_heads.shape[2]
    key_heads = key_piece.reshape(key_count, head_count, head_size)
    value_heads = value_piece.reshape(key_count, head_count, head_size)
    scores = (
        jnp.einsum("qhd,khd->hqk", query_heads, key_heads, preferred_element_type=jnp.float32)
        * inv_root
    )
    scores = jnp.where(mask_piece[None, None, :], scores, neg_large)
    new_top = jnp.maximum(row_top, jnp.max(scores, axis=2))
    weights = jnp.where(mask_piece[None, None, :], jnp.exp(scores - new_top[:, :, None]), 0.0)
    factor = jnp.exp(row_top - new_top)
    denominator = denominator * factor + jnp.sum(weights, axis=2)
    rounded = weights.astype(jnp.bfloat16)
    weighted = weighted * factor[:, :, None] + jnp.einsum(
        "hqk,khd->hqd", rounded, value_heads, preferred_element_type=jnp.float32
    )
    return (new_top, denominator, weighted)


def make_folder(query_heads, key_valid, inv_root):

    def fold_keys(running, shard_piece, start_row):
        key_piece, value_piece = shard_piece
        key_count = key_piece.shape[0]
        if key_count > 2 * key_block and key_count % key_block == 0:
            block_total = key_count // key_block

            def block_step(carried, block_items):
                return (
                    attend_update(
                        carried,
                        query_heads,
                        block_items[0],
                        block_items[1],
                        block_items[2],
                        inv_root,
                    ),
                    None,
                )

            stacked = (
                key_piece.reshape(block_total, key_block, key_piece.shape[1]),
                value_piece.reshape(block_total, key_block, value_piece.shape[1]),
                key_valid.reshape(block_total, key_block),
            )
            running, unused = lax.scan(block_step, running, stacked)
            return running
        return attend_update(running, query_heads, key_piece, value_piece, key_valid, inv_root)

    return fold_keys


def initial_state(query_rows, head_count, head_size):
    return (
        jnp.full((head_count, query_rows), neg_large, jnp.float32),
        jnp.zeros((head_count, query_rows), jnp.float32),
        jnp.zeros((head_count, query_rows, head_size), jnp.float32),
    )


def finish_state(running):
    row_top, denominator, weighted = running
    normalized = weighted / denominator[:, :, None]
    head_count, query_rows, head_size = normalized.shape
    return (
        jnp.transpose(normalized, (1, 0, 2))
        .reshape(query_rows, head_count * head_size)
        .astype(jnp.bfloat16)
    )


def per_device(
    tokens, positions, counts, timestep, time_in, time_out, ada_weight, qkv_weight, out_weight
):
    devices = lax.axis_size("patch")
    my_index = lax.axis_index("patch")
    local_rows = tokens.shape[0]
    model_width = tokens.shape[1]
    head_count = HEADS
    head_size = model_width // head_count
    inv_root = 1.0 / math.sqrt(head_size)
    features = time_features(timestep, time_in.shape[0])
    hidden_time = jax.nn.silu(
        jnp.dot(features, time_in, preferred_element_type=jnp.float32)
    ).astype(jnp.bfloat16)
    cond_part = jnp.dot(hidden_time, time_out, preferred_element_type=jnp.float32)
    activated = jax.nn.silu(cond_part).astype(jnp.bfloat16)
    partial_mod = jnp.dot(activated, ada_weight, preferred_element_type=jnp.float32)
    modulation = lax.psum(partial_mod, "patch")
    shift_mod = modulation[:, :model_width]
    scale_mod = modulation[:, model_width : 2 * model_width]
    gate_mod = modulation[:, 2 * model_width :]
    x_in = tokens.astype(jnp.float32) + position_table(positions, model_width)
    mean_value = jnp.mean(x_in, axis=1, keepdims=True)
    centered = x_in - mean_value
    variance = jnp.mean(centered * centered, axis=1, keepdims=True)
    normed = centered * lax.rsqrt(variance + 1e-06)
    modulated = (normed * (1.0 + scale_mod) + shift_mod).astype(jnp.bfloat16)
    counts_here = lax.dynamic_index_in_dim(counts, my_index, keepdims=False)
    row_ids = jnp.arange(local_rows, dtype=jnp.int32)
    row_valid = row_ids < counts_here
    projections = jnp.dot(modulated, qkv_weight, preferred_element_type=jnp.float32).astype(
        jnp.bfloat16
    )
    groups = devices // head_count
    part_rows = local_rows // groups
    query_split = projections[:, :model_width].reshape(groups, part_rows, head_count, head_size)
    query_send = jnp.transpose(query_split, (0, 2, 1, 3)).reshape(devices, part_rows, head_size)
    key_split = projections[:, model_width : 2 * model_width].reshape(
        local_rows, head_count, head_size
    )
    value_split = projections[:, 2 * model_width :].reshape(local_rows, head_count, head_size)
    pair_heads = jnp.transpose(jnp.concatenate([key_split, value_split], axis=2), (1, 0, 2))
    pair_send = jnp.broadcast_to(pair_heads[None], (groups, head_count, local_rows, 2 * head_size))
    pair_send = pair_send.reshape(devices, local_rows, 2 * head_size)
    got_query, got_pair = (
        lax.all_to_all(query_send, "patch", split_axis=0, concat_axis=0, tiled=True),
        lax.all_to_all(pair_send, "patch", split_axis=0, concat_axis=0, tiled=True),
    )
    query_rows = devices * part_rows
    query_heads = got_query.reshape(query_rows, 1, head_size)
    all_pairs = got_pair.reshape(devices * local_rows, 2 * head_size)
    key_valid = (jnp.arange(local_rows, dtype=jnp.int32)[None, :] < counts[:, None]).reshape(-1)
    folder = make_folder(query_heads, key_valid, inv_root)
    running = folder(
        initial_state(query_rows, 1, head_size),
        (all_pairs[:, :head_size], all_pairs[:, head_size:]),
        0,
    )
    head_result = finish_state(running).reshape(devices, part_rows, head_size)
    came_back = lax.all_to_all(head_result, "patch", split_axis=0, concat_axis=0, tiled=True)
    attended = jnp.transpose(
        came_back.reshape(groups, head_count, part_rows, head_size), (0, 2, 1, 3)
    )
    attended = attended.reshape(local_rows, model_width)
    projected = jnp.dot(attended, out_weight, preferred_element_type=jnp.float32)
    valid_column = row_valid.astype(jnp.float32)[:, None]
    return (x_in + gate_mod * projected * valid_column).astype(jnp.bfloat16)


def solution(mesh):
    placed = (
        P(("req", "patch"), None),
        P(None, ("req", "patch")),
        P("req"),
        P("req"),
        P(),
        P(None, "patch"),
        P("patch", None),
        P(),
        P(),
    )
    return jax.shard_map(
        per_device, mesh=mesh, in_specs=placed, out_specs=P(("req", "patch"), None), check_vma=False
    )
```

profile of v0, /device:TPU:0, one launch (start us, length us, event | category | flops | bytes accessed | tf_op | source)
XLA Modules:
  0.0 123.4 jit_solution(13335369351316423858)
XLA Ops:
  0.0 0.9 convert_bitcast_fusion
  0.9 0.6 multiply_cosine_fusion
  1.5 0.1 concatenate.13
  1.6 1.0 fusion.25
  2.7 1.1 multiply_reduce_fusion
  4.5 1.3 %convolution_reduce_fusion = f32[1152]{0:T(1024)S(1)} fusion(bf16[256,1]{0,1:T(2,128)(2,1)S(1)} %reshape.180, bf16[256,1152]{1,0:T(8,128)(2,1)} %param.13), kind=kOutput, calls=%fused_computation.15 | convolution fusion | flops 589824 | bytes 594944 | tf_op jit(solution)/shard_map/dot_general | solution.py:116
  5.8 1.6 %fusion.27 = f32[1,3456]{1,0:T(1,128)S(1)} fusion(bf16[72,3456]{1,0:T(8,128)(2,1)} %param.15, bf16[1152,1]{0,1:T(2,128)(2,1)S(1)} %reshape.182, bf16[1152,72]{0,1:T(8,128)(2,1)} %param.14), kind=kOutput, calls=%fused_computation.46 | convolution fusion | flops 663912 | bytes 679680 | tf_op jit(solution)/shard_map/dot_general | solution.py:120
  7.4 63.0 %psum.7 = f32[1,3456]{1,0:T(1,128)S(1)} all-reduce(f32[1,3456]{1,0:T(1,128)S(1)} %fusion.27), channel_id=1, replica_groups=mesh['req'=2,'patch'=16] {'patch'}, use_global_device_ids=true, to_apply=%region_0.1 | all-reduce | flops 3456 | bytes 27648 | tf_op jit(solution)/shard_map/psum | solution.py:121
  70.4 4.6 %convolution_convert_fusion = bf16[48,3456]{1,0:T(8,128)(2,1)S(1)} fusion(bf16[1152,3456]{1,0:T(8,128)(2,1)} %param.16, f32[1152]{0:T(1024)S(1)} %get-tuple-element.6, f32[1152]{0:T(1024)S(1)} %get-tuple-element.7, f32[48]{0:T(128)S(1)} %add_rsqrt_fusion, f32[48]{0:T(128)S(1)} %broadcast_multiply_fusion, f32[48,1152]{1,0:T(8,128)S(1)} %concatenate.13, ...), kind=kOutput, calls=%fused_computation | convolution fusion | flops 382758912 | bytes 8635776 | tf_op jit(solution)/shard_map/dot_general | solution.py:134
  75.0 0.7 fusion.38
  75.7 0.3 reshape.172
  76.1 0.7 copy.16
  76.8 3.5 %all-to-all-start = ((bf16[16,48,72]{2,1,0:T(8,128)(2,1)}), bf16[16,48,72]{2,1,0:T(8,128)(2,1)S(1)}, u32[]{:S(2)}, u32[]{:S(2)}) async-start(bf16[16,48,72]{2,1,0:T(8,128)(2,1)} %bitcast.38), calls=%async_computation | async-start | bytes 393216 | tf_op jit(solution)/shard_map/all_to_all | solution.py:149
  80.3 1.2 %reshape.175 = bf16[48,16,72]{2,1,0:T(8,128)(2,1)S(1)} reshape(bf16[48,1152]{1,0:T(8,128)(2,1)} %get-tuple-element.8) | data formatting | bytes 221184 | tf_op jit(solution)/shard_map/reshape | solution.py:141
  81.6 0.7 copy.11
  82.3 0.3 reshape.176
  82.7 1.8 %maximum_bitcast_fusion = bf16[16,48,144]{2,1,0:T(8,128)(2,1)} fusion(bf16[48,16,72]{2,0,1:T(8,128)(2,1)S(1)} %copy.12, bf16[48,16,72]{2,0,1:T(8,128)(2,1)} %copy.11), kind=kLoop, calls=%fused_computation.17 | loop fusion | flops 442368 | bytes 442368 | tf_op jit(solution)/shard_map/transpose | solution.py:145
  84.5 4.7 %all-to-all-done = bf16[16,48,72]{2,1,0:T(8,128)(2,1)S(1)} async-done(((bf16[16,48,72]{2,1,0:T(8,128)(2,1)}), bf16[16,48,72]{2,1,0:T(8,128)(2,1)S(1)}, u32[]{:S(2)}, u32[]{:S(2)}) %all-to-all-start) | async-done | bytes 110624 | tf_op jit(solution)/shard_map/all_to_all | solution.py:149
  89.2 0.7 copy-done.2
  89.9 3.6 %all-to-all-start.1 = ((bf16[16,48,144]{2,1,0:T(8,128)(2,1)}), bf16[16,48,144]{2,1,0:T(8,128)(2,1)S(1)}, u32[]{:S(2)}, u32[]{:S(2)}) async-start(bf16[16,48,144]{2,1,0:T(8,128)(2,1)} %maximum_bitcast_fusion), calls=%async_computation.1 | async-start | bytes 786432 | tf_op jit(solution)/shard_map/all_to_all | solution.py:150
  93.6 0.1 lt.37
  93.6 12.0 %all-to-all-done.1 = bf16[16,48,144]{2,1,0:T(8,128)(2,1)S(1)} async-done(((bf16[16,48,144]{2,1,0:T(8,128)(2,1)}), bf16[16,48,144]{2,1,0:T(8,128)(2,1)S(1)}, u32[]{:S(2)}, u32[]{:S(2)}) %all-to-all-start.1) | async-done | bytes 221216 | tf_op jit(solution)/shard_map/all_to_all | solution.py:150
  105.6 1.5 %fusion.3 = (f32[768]{0:T(1024)S(1)}, f32[768,768]{0,1:T(8,128)S(1)}) fusion(pred[768]{0:T(1024)(128)(4,1)S(1)} %lt.37, bf16[768,72]{1,0:T(8,128)(2,1)} %bitcast.41, bf16[768,144]{1,0:T(8,128)(2,1)S(1)} %bitcast.39), kind=kOutput, calls=%fused_computation.7 | convolution fusion | flops 86703360 | bytes 2670592 | tf_op jit(solution)/shard_map/qhd,khd->hqk/dot_general | solution.py:37
  107.1 0.6 fusion.4
  107.7 0.8 fusion.15
  108.6 0.8 copy.13
  109.4 3.5 %all-to-all-start.2 = ((bf16[16,48,72]{2,1,0:T(8,128)(2,1)}), bf16[16,48,72]{2,1,0:T(8,128)(2,1)S(1)}, u32[]{:S(2)}, u32[]{:S(2)}) async-start(bf16[16,48,72]{2,1,0:T(8,128)(2,1)} %bitcast.10), calls=%async_computation.2 | async-start | bytes 393216 | tf_op jit(solution)/shard_map/all_to_all | solution.py:163
  112.9 0.6 dynamic_slice.4
  113.5 0.6 compare_convert_fusion
  114.1 7.7 %all-to-all-done.2 = bf16[16,48,72]{2,1,0:T(8,128)(2,1)S(1)} async-done(((bf16[16,48,72]{2,1,0:T(8,128)(2,1)}), bf16[16,48,72]{2,1,0:T(8,128)(2,1)S(1)}, u32[]{:S(2)}, u32[]{:S(2)}) %all-to-all-start.2) | async-done | bytes 110624 | tf_op jit(solution)/shard_map/all_to_all | solution.py:163
  121.9 0.2 reshape.179
  122.1 1.2 %fusion.2 = bf16[48,1152]{1,0:T(8,128)(2,1)} fusion(bf16[48,1152]{1,0:T(8,128)(2,1)S(1)} %reshape.179, bf16[1152,1152]{1,0:T(8,128)(2,1)S(1)} %copy-done, f32[48]{0:T(128)S(1)} %compare_convert_fusion, f32[1152]{0:T(1024)S(1)} %get-tuple-element.5, f32[48,1152]{1,0:T(8,128)S(1)} %concatenate.13, bf16[48,1152]{1,0:T(8,128)(2,1)S(1)} %copy-done.1), kind=kOutput, calls=%fused_computation.6 | convolution fusion | flops 127733760 | bytes 3211968 | tf_op jit(solution)/shard_map/dot_general | solution.py:168
  (21 shorter events, 0.4 us)
Async XLA Ops:
  0.0 122.1 %copy-start = (bf16[1152,1152]{1,0:T(8,128)(2,1)S(1)}, bf16[1152,1152]{1,0:T(8,128)(2,1)}, u32[]{:S(2)}) copy-start(bf16[1152,1152]{1,0:T(8,128)(2,1)} %param.17) | copy-start | bytes 7962628
  0.0 70.4 %copy-start.1 = (bf16[48,1152]{1,0:T(8,128)(2,1)S(1)}, bf16[48,1152]{1,0:T(8,128)(2,1)}, u32[]{:S(2)}) copy-start(bf16[48,1152]{1,0:T(8,128)(2,1)} %param.9) | copy-start | bytes 331780
  75.0 18.4 %copy-start.3 = (s32[16]{0:T(128)S(1)}, s32[16]{0:T(128)}, u32[]{:S(2)}) copy-start(s32[16]{0:T(128)} %param.11) | copy-start | bytes 196
  76.8 12.5 %all-to-all-start = ((bf16[16,48,72]{2,1,0:T(8,128)(2,1)}), bf16[16,48,72]{2,1,0:T(8,128)(2,1)S(1)}, u32[]{:S(2)}, u32[]{:S(2)}) async-start(bf16[16,48,72]{2,1,0:T(8,128)(2,1)} %bitcast.38), calls=%async_computation | async-start | bytes 393216 | tf_op jit(solution)/shard_map/all_to_all | solution.py:149
  89.2 0.7 copy-start.2
  89.9 15.7 %all-to-all-start.1 = ((bf16[16,48,144]{2,1,0:T(8,128)(2,1)}), bf16[16,48,144]{2,1,0:T(8,128)(2,1)S(1)}, u32[]{:S(2)}, u32[]{:S(2)}) async-start(bf16[16,48,144]{2,1,0:T(8,128)(2,1)} %maximum_bitcast_fusion), calls=%async_computation.1 | async-start | bytes 786432 | tf_op jit(solution)/shard_map/all_to_all | solution.py:150
  109.4 12.5 %all-to-all-start.2 = ((bf16[16,48,72]{2,1,0:T(8,128)(2,1)}), bf16[16,48,72]{2,1,0:T(8,128)(2,1)S(1)}, u32[]{:S(2)}, u32[]{:S(2)}) async-start(bf16[16,48,72]{2,1,0:T(8,128)(2,1)} %bitcast.10), calls=%async_computation.2 | async-start | bytes 393216 | tf_op jit(solution)/shard_map/all_to_all | solution.py:163
where the time goes:
time: 124 us; the launch traced here: 123 us
  blocking collectives  63 us (51%)
  waiting for transfers between devices  24.3 us (20%)
  matrix products  11 us (9%)
  starting transfers between devices  10.6 us (9%)
  other arithmetic  6.94 us (6%)
  local copies, waits for them, and re-layouts  6.71 us (5%)
    psum x1, blocking collectives, per_device(): modulation = lax.psum(partial_mod, 'patch')  63 us
    all_to_all x1, waiting for transfers between devices, per_device(): lax.all_to_all(pair_send, 'patch', split_axis=0, concat_axis=0, tiled=True)  12 us
    all_to_all x1, waiting for transfers between devices, per_device(): lax.all_to_all(head_result, 'patch', split_axis=0, concat_axis=0, tiled=T...  7.68 us
    all_to_all x1, waiting for transfers between devices, per_device(): lax.all_to_all(query_send, 'patch', split_axis=0, concat_axis=0, tiled=True)  4.69 us
    dot_general x1, matrix products, per_device(): jnp.dot(modulated, qkv_weight, preferred_element_type=jnp.float32)  4.6 us
    all_to_all x1, starting transfers between devices, per_device(): lax.all_to_all(pair_send, 'patch', split_axis=0, concat_axis=0, tiled=True)  3.55 us
    all_to_all x1, starting transfers between devices, per_device(): lax.all_to_all(query_send, 'patch', split_axis=0, concat_axis=0, tiled=True)  3.52 us
    all_to_all x1, starting transfers between devices, per_device(): lax.all_to_all(head_result, 'patch', split_axis=0, concat_axis=0, tiled=T...  3.52 us
  transfers between devices with their start and end apart: 3, of which 3 were waited for; matrix products, arithmetic and copies ran while one was open for 5% of the time, Pallas kernels for 0%

commit v1 on v0

--- a/solution.py
+++ b/solution.py
@@ -118,7 +118,8 @@
     cond_part = jnp.dot(hidden_time, time_out, preferred_element_type=jnp.float32)
     activated = jax.nn.silu(cond_part).astype(jnp.bfloat16)
     partial_mod = jnp.dot(activated, ada_weight, preferred_element_type=jnp.float32)
-    modulation = lax.psum(partial_mod, "patch")
+    parts = lax.all_gather(partial_mod, "patch", axis=0, tiled=False)
+    modulation = parts.sum(axis=0)
     shift_mod = modulation[:, :model_width]
     scale_mod = modulation[:, model_width : 2 * model_width]
     gate_mod = modulation[:, 2 * model_width :]

time: 124 us -> 84.9 us (0.68)
  blocking collectives: 63 us -> 23.7 us
    psum x1 -> x0, blocking collectives: 63 us -> none  [per_device(): modulation = lax.psum(partial_mod, 'patch')]
    all_gather x0 -> x1, blocking collectives: none -> 23.7 us  [per_device(): parts = lax.all_gather(partial_mod, 'patch', axis=0, tiled=False)]
  transfers between devices with their start and end apart: 3 -> 3, of which waited for: 3 -> 3; matrix products, arithmetic and copies ran while one was open for 5% -> 7% of each run, Pallas kernels for 0% -> 0%
where the time goes in v1:
time: 84.9 us; the launch traced here: 84.3 us
  waiting for transfers between devices  24.3 us (29%)
  blocking collectives  23.7 us (28%)
  matrix products  11 us (13%)
  starting transfers between devices  10.6 us (12%)
  other arithmetic  7.09 us (8%)
  local copies, waits for them, and re-layouts  6.72 us (8%)
  between operations  0.88 us (1%)
    all_gather x1, blocking collectives, per_device(): parts = lax.all_gather(partial_mod, 'patch', axis=0, tiled=False)  23.7 us
    all_to_all x1, waiting for transfers between devices, per_device(): lax.all_to_all(pair_send, 'patch', split_axis=0, concat_axis=0, tiled=True)  12 us
    all_to_all x1, waiting for transfers between devices, per_device(): lax.all_to_all(head_result, 'patch', split_axis=0, concat_axis=0, tiled=T...  7.68 us
    all_to_all x1, waiting for transfers between devices, per_device(): lax.all_to_all(query_send, 'patch', split_axis=0, concat_axis=0, tiled=True)  4.69 us
    dot_general x1, matrix products, per_device(): jnp.dot(modulated, qkv_weight, preferred_element_type=jnp.float32)  4.61 us
    all_to_all x1, starting transfers between devices, per_device(): lax.all_to_all(pair_send, 'patch', split_axis=0, concat_axis=0, tiled=True)  3.55 us
    all_to_all x1, starting transfers between devices, per_device(): lax.all_to_all(query_send, 'patch', split_axis=0, concat_axis=0, tiled=True)  3.52 us
    all_to_all x1, starting transfers between devices, per_device(): lax.all_to_all(head_result, 'patch', split_axis=0, concat_axis=0, tiled=T...  3.52 us
  transfers between devices with their start and end apart: 3, of which 3 were waited for; matrix products, arithmetic and copies ran while one was open for 7% of the time, Pallas kernels for 0%

profile of v1, /device:TPU:0, one launch (start us, length us, event | category | flops | bytes accessed | tf_op | source)
XLA Modules:
  0.0 84.3 jit_solution(7440912104920625258)
XLA Ops:
  0.0 0.9 %convert_bitcast_fusion = (f32[48]{0:T(128)S(1)}, f32[48]{0:T(128)S(1)}) fusion(s32[2,48]{1,0:T(2,128)} %param.10), kind=kLoop, calls=%fused_computation.55 | loop fusion | flops 96 | bytes 768 | tf_op jit(solution)/shard_map/convert_element_type | solution.py:23
  0.9 0.6 multiply_cosine_fusion
  1.5 0.1 concatenate.13
  1.6 1.0 %fusion.25 = f32[48]{0:T(128)S(1)} fusion(f32[48,1152]{1,0:T(8,128)S(1)} %concatenate.13, bf16[48,1152]{1,0:T(8,128)(2,1)} %param.9), kind=kLoop, calls=%fused_computation.34 | loop fusion | flops 165840 | bytes 331968 | tf_op jit(solution)/shard_map/reduce_sum | solution.py:127
  2.7 1.1 %multiply_reduce_fusion = f32[48]{0:T(128)S(1)} fusion(f32[48]{0:T(128)S(1)} %broadcast_multiply_fusion, f32[48,1152]{1,0:T(8,128)S(1)} %concatenate.13, bf16[48,1152]{1,0:T(8,128)(2,1)} %param.9), kind=kLoop, calls=%fused_computation.20 | loop fusion | flops 276432 | bytes 332160 | tf_op jit(solution)/shard_map/reduce_sum | solution.py:129
  4.5 1.3 %convolution_reduce_fusion = f32[1152]{0:T(1024)S(1)} fusion(bf16[256,1]{0,1:T(2,128)(2,1)S(1)} %reshape.187, bf16[256,1152]{1,0:T(8,128)(2,1)} %param.13), kind=kOutput, calls=%fused_computation.16 | convolution fusion | flops 589824 | bytes 594944 | tf_op jit(solution)/shard_map/dot_general | solution.py:116
  5.8 1.6 %convolution_bitcast_fusion = f32[1,1,3456]{2,1,0:T(1,128)S(1)} fusion(bf16[72,3456]{1,0:T(8,128)(2,1)} %param.15, bf16[1152,1]{0,1:T(2,128)(2,1)S(1)} %reshape.189, bf16[1152,72]{0,1:T(8,128)(2,1)} %param.14), kind=kOutput, calls=%fused_computation.1 | convolution fusion | flops 663912 | bytes 679680 | tf_op jit(solution)/shard_map/dot_general | solution.py:120
  7.4 23.7 %all-gather.1 = f32[16,1,3456]{2,1,0:T(1,128)S(1)} all-gather(f32[1,1,3456]{2,1,0:T(1,128)S(1)} %convolution_bitcast_fusion), channel_id=2, replica_groups=mesh['req'=2,'patch'=16] {'patch'}, dimensions={0}, use_global_device_ids=true | all-gather | bytes 235008 | tf_op jit(solution)/shard_map/all_gather | solution.py:121
  31.1 0.1 reduce.5
  31.3 4.6 %convolution_convert_fusion = bf16[48,3456]{1,0:T(8,128)(2,1)S(1)} fusion(bf16[1152,3456]{1,0:T(8,128)(2,1)} %param.16, f32[1152]{0:T(1024)S(1)} %get-tuple-element.6, f32[1152]{0:T(1024)S(1)} %get-tuple-element.7, f32[48]{0:T(128)S(1)} %add_rsqrt_fusion, f32[48]{0:T(128)S(1)} %broadcast_multiply_fusion, f32[48,1152]{1,0:T(8,128)S(1)} %concatenate.13, ...), kind=kOutput, calls=%fused_computation | convolution fusion | flops 382758912 | bytes 8635776 | tf_op jit(solution)/shard_map/dot_general | solution.py:135
  35.9 0.7 fusion.37
  36.6 0.3 reshape.174
  37.0 0.7 copy.21
  37.7 3.5 %all-to-all-start = ((bf16[16,48,72]{2,1,0:T(8,128)(2,1)}), bf16[16,48,72]{2,1,0:T(8,128)(2,1)S(1)}, u32[]{:S(2)}, u32[]{:S(2)}) async-start(bf16[16,48,72]{2,1,0:T(8,128)(2,1)} %bitcast.40), calls=%async_computation | async-start | bytes 393216 | tf_op jit(solution)/shard_map/all_to_all | solution.py:150
  41.2 1.2 %reshape.177 = bf16[48,16,72]{2,1,0:T(8,128)(2,1)S(1)} reshape(bf16[48,1152]{1,0:T(8,128)(2,1)} %get-tuple-element.8) | data formatting | bytes 221184 | tf_op jit(solution)/shard_map/reshape | solution.py:142
  42.5 0.7 copy.16
  43.2 0.3 reshape.178
  43.6 1.8 %maximum_bitcast_fusion = bf16[16,48,144]{2,1,0:T(8,128)(2,1)} fusion(bf16[48,16,72]{2,0,1:T(8,128)(2,1)S(1)} %copy.17, bf16[48,16,72]{2,0,1:T(8,128)(2,1)} %copy.16), kind=kLoop, calls=%fused_computation.18 | loop fusion | flops 442368 | bytes 442368 | tf_op jit(solution)/shard_map/transpose | solution.py:146
  45.4 4.7 %all-to-all-done = bf16[16,48,72]{2,1,0:T(8,128)(2,1)S(1)} async-done(((bf16[16,48,72]{2,1,0:T(8,128)(2,1)}), bf16[16,48,72]{2,1,0:T(8,128)(2,1)S(1)}, u32[]{:S(2)}, u32[]{:S(2)}) %all-to-all-start) | async-done | bytes 110624 | tf_op jit(solution)/shard_map/all_to_all | solution.py:150
  50.1 0.7 copy-done.2
  50.8 3.6 %all-to-all-start.1 = ((bf16[16,48,144]{2,1,0:T(8,128)(2,1)}), bf16[16,48,144]{2,1,0:T(8,128)(2,1)S(1)}, u32[]{:S(2)}, u32[]{:S(2)}) async-start(bf16[16,48,144]{2,1,0:T(8,128)(2,1)} %maximum_bitcast_fusion), calls=%async_computation.1 | async-start | bytes 786432 | tf_op jit(solution)/shard_map/all_to_all | solution.py:151
  54.5 12.0 %all-to-all-done.1 = bf16[16,48,144]{2,1,0:T(8,128)(2,1)S(1)} async-done(((bf16[16,48,144]{2,1,0:T(8,128)(2,1)}), bf16[16,48,144]{2,1,0:T(8,128)(2,1)S(1)}, u32[]{:S(2)}, u32[]{:S(2)}) %all-to-all-start.1) | async-done | bytes 221216 | tf_op jit(solution)/shard_map/all_to_all | solution.py:151
  66.5 1.5 %fusion.3 = (f32[768]{0:T(1024)S(1)}, f32[768,768]{0,1:T(8,128)S(1)}) fusion(pred[768]{0:T(1024)(128)(4,1)S(1)} %lt.37, bf16[768,72]{1,0:T(8,128)(2,1)} %bitcast.43, bf16[768,144]{1,0:T(8,128)(2,1)S(1)} %bitcast.41), kind=kOutput, calls=%fused_computation.8 | convolution fusion | flops 86703360 | bytes 2670592 | tf_op jit(solution)/shard_map/qhd,khd->hqk/dot_general | solution.py:37
  68.0 0.6 fusion.4
  68.6 0.8 fusion.15
  69.5 0.8 copy.18
  70.3 3.5 %all-to-all-start.2 = ((bf16[16,48,72]{2,1,0:T(8,128)(2,1)}), bf16[16,48,72]{2,1,0:T(8,128)(2,1)S(1)}, u32[]{:S(2)}, u32[]{:S(2)}) async-start(bf16[16,48,72]{2,1,0:T(8,128)(2,1)} %bitcast.10), calls=%async_computation.2 | async-start | bytes 393216 | tf_op jit(solution)/shard_map/all_to_all | solution.py:164
  73.8 0.6 dynamic_slice.4
  74.4 0.6 compare_convert_fusion
  75.0 7.7 %all-to-all-done.2 = bf16[16,48,72]{2,1,0:T(8,128)(2,1)S(1)} async-done(((bf16[16,48,72]{2,1,0:T(8,128)(2,1)}), bf16[16,48,72]{2,1,0:T(8,128)(2,1)S(1)}, u32[]{:S(2)}, u32[]{:S(2)}) %all-to-all-start.2) | async-done | bytes 110624 | tf_op jit(solution)/shard_map/all_to_all | solution.py:164
  82.8 0.2 reshape.181
  83.0 1.2 %fusion.2 = bf16[48,1152]{1,0:T(8,128)(2,1)} fusion(bf16[48,1152]{1,0:T(8,128)(2,1)S(1)} %reshape.181, bf16[1152,1152]{1,0:T(8,128)(2,1)S(1)} %copy-done, f32[48]{0:T(128)S(1)} %compare_convert_fusion, f32[1152]{0:T(1024)S(1)} %get-tuple-element.5, f32[48,1152]{1,0:T(8,128)S(1)} %concatenate.13, bf16[48,1152]{1,0:T(8,128)(2,1)S(1)} %copy-done.1), kind=kOutput, calls=%fused_computation.7 | convolution fusion | flops 127733760 | bytes 3211968 | tf_op jit(solution)/shard_map/dot_general | solution.py:169
  (23 shorter events, 0.5 us)
Async XLA Ops:
  0.0 83.0 %copy-start = (bf16[1152,1152]{1,0:T(8,128)(2,1)S(1)}, bf16[1152,1152]{1,0:T(8,128)(2,1)}, u32[]{:S(2)}) copy-start(bf16[1152,1152]{1,0:T(8,128)(2,1)} %param.17) | copy-start | bytes 7962628
  0.0 31.3 %copy-start.1 = (bf16[48,1152]{1,0:T(8,128)(2,1)S(1)}, bf16[48,1152]{1,0:T(8,128)(2,1)}, u32[]{:S(2)}) copy-start(bf16[48,1152]{1,0:T(8,128)(2,1)} %param.9) | copy-start | bytes 331780
  35.9 18.4 %copy-start.3 = (s32[16]{0:T(128)S(1)}, s32[16]{0:T(128)}, u32[]{:S(2)}) copy-start(s32[16]{0:T(128)} %param.11) | copy-start | bytes 196
  37.7 12.5 %all-to-all-start = ((bf16[16,48,72]{2,1,0:T(8,128)(2,1)}), bf16[16,48,72]{2,1,0:T(8,128)(2,1)S(1)}, u32[]{:S(2)}, u32[]{:S(2)}) async-start(bf16[16,48,72]{2,1,0:T(8,128)(2,1)} %bitcast.40), calls=%async_computation | async-start | bytes 393216 | tf_op jit(solution)/shard_map/all_to_all | solution.py:150
  50.1 0.7 copy-start.2
  50.8 15.7 %all-to-all-start.1 = ((bf16[16,48,144]{2,1,0:T(8,128)(2,1)}), bf16[16,48,144]{2,1,0:T(8,128)(2,1)S(1)}, u32[]{:S(2)}, u32[]{:S(2)}) async-start(bf16[16,48,144]{2,1,0:T(8,128)(2,1)} %maximum_bitcast_fusion), calls=%async_computation.1 | async-start | bytes 786432 | tf_op jit(solution)/shard_map/all_to_all | solution.py:151
  70.3 12.5 %all-to-all-start.2 = ((bf16[16,48,72]{2,1,0:T(8,128)(2,1)}), bf16[16,48,72]{2,1,0:T(8,128)(2,1)S(1)}, u32[]{:S(2)}, u32[]{:S(2)}) async-start(bf16[16,48,72]{2,1,0:T(8,128)(2,1)} %bitcast.10), calls=%async_computation.2 | async-start | bytes 393216 | tf_op jit(solution)/shard_map/all_to_all | solution.py:164
